TPU v7x, 32 devices: a whole 2x2x4 slice. The times are simulated.
32 devices in a mesh: head: 2 (over y), blk: 16 (over z, x, core).
Axes of the slice: x: 2, y: 2, z: 4, core: 2. Of those that a mesh axis runs over, the one named last changes fastest.
Arguments:
- query_rows: bfloat16 [16, 144, 3072], P('blk', 'head'), may hold values from -6 to 6
- key_rows: bfloat16 [16, 144, 3072], P('blk', 'head'), may hold values from -6 to 6
- value_rows: bfloat16 [16, 144, 3072], P('blk', 'head'), may hold values from -6 to 6
- query_tangent: bfloat16 [16, 144, 3072], P('blk', 'head'), may hold values from -6 to 6
- key_tangent: bfloat16 [16, 144, 3072], P('blk', 'head'), may hold values from -6 to 6
- value_tangent: bfloat16 [16, 144, 3072], P('blk', 'head'), may hold values from -6 to 6
- query_gain: float32 [128], replicated, may hold values from 1 to 6
- key_gain: float32 [128], replicated, may hold values from 1 to 6
Outputs:
- attended: bfloat16 [16, 144, 3072], P('blk', 'head')
- attended_tangent: bfloat16 [16, 144, 3072], P('blk', 'head')
All inputs are finite; a program needn't handle non-finite values.
Results may differ from a plain program's by a relative error of at most 0.014.
The roundings to bfloat16 on the way count: a program that leaves them out, or rounds other values in their place, can miss the bound.
Values may be sent and summed in bfloat16 or wider, within the bound.
A program may use at most 64 MiB of HBM per device.

v0:
```python
import math

import jax
import jax.numpy as jnp
from jax import lax
from jax.sharding import PartitionSpec as P

HD = 128
TXT = 512
GRID_W = 64
GROUP = 16


EPSILON = 1e-06
THETA = 10000.0


def passed_along(block, axis, distance):
    devices = range(lax.axis_size(axis))
    route = [((i - distance) % len(devices), i) for i in devices]
    return lax.ppermute(block, axis, route)


def rotation(first, count, head_dim):
    block_offsets = first + jnp.arange(count, dtype=jnp.int32)
    is_image = block_offsets >= TXT
    patch = jnp.maximum(block_offsets - TXT, 0)
    row_id = jnp.where(is_image, patch // GRID_W, 0).astype(jnp.float32)
    column_id = jnp.where(is_image, patch % GRID_W, 0).astype(jnp.float32)
    leading = head_dim // 8
    lateral = (head_dim - leading) // 2
    exponent = jnp.arange(lateral // 2, dtype=jnp.float32) * (2.0 / lateral)
    frequency = jnp.exp(-math.log(THETA) * exponent)
    angles = jnp.concatenate(
        [
            jnp.zeros((count, leading // 2), jnp.float32),
            row_id[:, None] * frequency[None, :],
            column_id[:, None] * frequency[None, :],
        ],
        axis=1,
    )
    angles = jnp.repeat(angles, 2, axis=1)
    return (jnp.cos(angles), jnp.sin(angles))


def rotation_partner(head_dim):
    across = jnp.arange(head_dim, dtype=jnp.int32)
    lower = across[:, None]
    upper = across[None, :]
    forward = ((upper == lower + 1) & (lower % 2 == 0)).astype(jnp.float32)
    backward = ((lower == upper + 1) & (upper % 2 == 0)).astype(jnp.float32)
    return forward - backward


def normalize(raw, tangent, gain, cosine, sine, partner):
    values = raw.astype(jnp.float32)
    motion = tangent.astype(jnp.float32)
    inverse = lax.rsqrt(jnp.mean(values * values, axis=-1, keepdims=True) + EPSILON)
    coupling = jnp.mean(values * motion, axis=-1, keepdims=True)
    normed = values * inverse * gain
    normalized_tangent = gain * (motion * inverse - values * inverse * inverse * inverse * coupling)

    def rotate(feature_field):
        return (
            feature_field * cosine
            + jnp.dot(feature_field, partner, precision=lax.Precision.HIGHEST) * sine
        )

    return (rotate(normed).astype(jnp.bfloat16), rotate(normalized_tangent).astype(jnp.bfloat16))


def local(
    query_rows,
    key_rows,
    value_rows,
    query_tangent,
    key_tangent,
    value_tangent,
    query_gain,
    key_gain,
):
    arrived = (
        lax.all_to_all(query_rows, "head", split_axis=2, concat_axis=1, tiled=True),
        lax.all_to_all(key_rows, "head", split_axis=2, concat_axis=1, tiled=True),
        lax.all_to_all(value_rows, "head", split_axis=2, concat_axis=1, tiled=True),
        lax.all_to_all(query_tangent, "head", split_axis=2, concat_axis=1, tiled=True),
        lax.all_to_all(key_tangent, "head", split_axis=2, concat_axis=1, tiled=True),
        lax.all_to_all(value_tangent, "head", split_axis=2, concat_axis=1, tiled=True),
    )
    rows_here = arrived[0].shape[1]
    local_width = arrived[0].shape[2]
    heads_here = local_width // HD
    images = lax.axis_size("blk") // GROUP
    place = lax.axis_index("blk") // images

    def split_heads(feature_field):
        return feature_field[0].reshape(rows_here, heads_here, HD)

    cosine, sine = rotation(place * rows_here, rows_here, HD)
    cosine = cosine[:, None, :]
    sine = sine[:, None, :]
    partner = rotation_partner(HD)
    query_hat, query_dot = normalize(
        split_heads(arrived[0]), split_heads(arrived[3]), query_gain, cosine, sine, partner
    )
    key_hat, key_dot = normalize(
        split_heads(arrived[1]), split_heads(arrived[4]), key_gain, cosine, sine, partner
    )
    own_block = jnp.stack(
        [
            key_hat.reshape(rows_here, local_width),
            arrived[2][0],
            key_dot.reshape(rows_here, local_width),
            arrived[5][0],
        ],
        axis=0,
    )
    scale = 1.0 / math.sqrt(HD)
    query_pair = jnp.concatenate([query_dot, query_hat], axis=2)

    def absorb_segment(state, key_block):
        peak, total, drift, summed, summed_dot = state
        count = key_block.shape[1]
        block_key = key_block[0].reshape(count, heads_here, HD)
        block_value = key_block[1].reshape(count, heads_here, HD)
        block_key_dot = key_block[2].reshape(count, heads_here, HD)
        block_value_dot = key_block[3].reshape(count, heads_here, HD)
        logit_scores = (
            jnp.einsum("qhd,khd->hqk", query_hat, block_key, preferred_element_type=jnp.float32)
            * scale
        )
        key_pair = jnp.concatenate([block_key, block_key_dot], axis=2)
        score_dot = (
            jnp.einsum("qhd,khd->hqk", query_pair, key_pair, preferred_element_type=jnp.float32)
            * scale
        )
        new_peak = jnp.maximum(peak, jnp.max(logit_scores, axis=2, keepdims=True))
        rescale = jnp.exp(peak - new_peak)
        weights = jnp.exp(logit_scores - new_peak)
        product = weights * score_dot
        total = total * rescale + jnp.sum(weights, axis=2, keepdims=True)
        drift = drift * rescale + jnp.sum(product, axis=2, keepdims=True)
        low_weights = weights.astype(jnp.bfloat16)
        low_product = product.astype(jnp.bfloat16)
        summed = summed * rescale + jnp.einsum(
            "hqk,khd->hqd", low_weights, block_value, preferred_element_type=jnp.float32
        )
        summed_dot = (
            summed_dot * rescale
            + jnp.einsum(
                "hqk,khd->hqd", low_weights, block_value_dot, preferred_element_type=jnp.float32
            )
            + jnp.einsum(
                "hqk,khd->hqd", low_product, block_value, preferred_element_type=jnp.float32
            )
        )
        return (new_peak, total, drift, summed, summed_dot)

    def absorb(state, key_block):
        count = key_block.shape[1]
        span = 2 * rows_here
        return absorb_segment(state, key_block)

    state = (
        jnp.full((heads_here, rows_here, 1), -jnp.inf, jnp.float32),
        jnp.zeros((heads_here, rows_here, 1), jnp.float32),
        jnp.zeros((heads_here, rows_here, 1), jnp.float32),
        jnp.zeros((heads_here, rows_here, HD), jnp.float32),
        jnp.zeros((heads_here, rows_here, HD), jnp.float32),
    )

    def pass_on(key_block):
        return passed_along(key_block, "blk", images)

    def pair_step(counter, carry):
        carried, current = carry
        following = pass_on(current)
        carried = absorb(carried, jnp.concatenate([current, following], axis=1))
        current = pass_on(following)
        return (carried, current)

    state, current = lax.fori_loop(0, GROUP // 2 - 1, pair_step, (state, own_block))
    following = pass_on(current)
    state = absorb(state, jnp.concatenate([current, following], axis=1))
    peak, total, drift, summed, summed_dot = state
    attention_output = summed / total
    output_tangent = (summed_dot - drift / total * summed) / total
    attention_output = (
        attention_output.transpose(1, 0, 2)
        .reshape(rows_here, local_width)
        .astype(jnp.bfloat16)[None]
    )
    output_tangent = (
        output_tangent.transpose(1, 0, 2).reshape(rows_here, local_width).astype(jnp.bfloat16)[None]
    )
    returned = (
        lax.all_to_all(attention_output, "head", split_axis=1, concat_axis=2, tiled=True),
        lax.all_to_all(output_tangent, "head", split_axis=1, concat_axis=2, tiled=True),
    )
    return (returned[0], returned[1])


def solution(mesh):
    in_specs = (
        P("blk", "head", None),
        P("blk", "head", None),
        P("blk", "head", None),
        P("blk", "head", None),
        P("blk", "head", None),
        P("blk", "head", None),
        P(),
        P(),
    )
    out_specs = (P("blk", "head", None), P("blk", "head", None))
    return jax.shard_map(local, mesh=mesh, in_specs=in_specs, out_specs=out_specs, check_vma=False)
```

profile of v0, /device:TPU:0, one launch (start us, length us, event | category | flops | bytes accessed | tf_op | source)
XLA Modules:
  0.0 685.8 jit_solution(4280245058798378353)
XLA Ops:
  0.6 3.6 copy.162
  4.8 17.0 %reduce.2 = bf16[3072,72]{1,0:T(8,128)(2,1)S(1)} reduce(bf16[3072,1,72]{2,1,0:T(2,128)(2,1)S(1)} %bitcast.161, bf16[]{:T(256)} %broadcast.317), dimensions={1}, to_apply=%bitcast.107.reduce_sub_computation | reduce | bytes 884738
  24.1 4.4 all-to-all-start
  30.5 17.0 %reduce.1 = bf16[3072,72]{1,0:T(8,128)(2,1)S(1)} reduce(bf16[3072,1,72]{2,1,0:T(2,128)(2,1)S(1)} %bitcast.162, bf16[]{:T(256)} %broadcast.317), dimensions={1}, to_apply=%bitcast.105.reduce_sub_computation | reduce | bytes 884738
  52.5 17.2 %reduce.3 = bf16[3072,72]{1,0:T(8,128)(2,1)S(1)} reduce(bf16[3072,1,72]{2,1,0:T(2,128)(2,1)S(1)} %bitcast.163, bf16[]{:T(256)} %broadcast.317), dimensions={1}, to_apply=%bitcast.109.reduce_sub_computation | reduce | bytes 884738
  73.9 17.0 %reduce = bf16[3072,72]{1,0:T(8,128)(2,1)S(1)} reduce(bf16[3072,1,72]{2,1,0:T(2,128)(2,1)S(1)} %bitcast.164, bf16[]{:T(256)} %broadcast.317), dimensions={1}, to_apply=%bitcast.103.reduce_sub_computation | reduce | bytes 884738
  90.9 2.7 reshape.172
  95.4 17.0 %reduce.4 = bf16[3072,72]{1,0:T(8,128)(2,1)S(1)} reduce(bf16[3072,1,72]{2,1,0:T(2,128)(2,1)S(1)} %bitcast.165, bf16[]{:T(256)} %broadcast.317), dimensions={1}, to_apply=%bitcast.111.reduce_sub_computation | reduce | bytes 884738
  116.6 17.1 %reduce.5 = bf16[3072,72]{1,0:T(8,128)(2,1)S(1)} reduce(bf16[3072,1,72]{2,1,0:T(2,128)(2,1)S(1)} %bitcast.166, bf16[]{:T(256)} %broadcast.317), dimensions={1}, to_apply=%bitcast.113.reduce_sub_computation | reduce | bytes 884738
  136.8 4.2 all-to-all-start.2
  141.0 3.7 reshape.177
  149.0 4.2 all-to-all-start.1
  153.1 3.7 reshape.175
  162.1 3.7 all-to-all-start.3
  169.3 3.5 all-to-all-done.3
  172.8 4.2 all-to-all-start.4
  179.7 3.7 reshape.179
  186.1 2.8 reshape.173
  191.5 4.6 all-to-all-start.5
  196.1 3.7 reshape.181
  203.2 3.7 reshape.183
  219.2 393.0 %while.21 = (s32[]{:T(128)}, f32[12,144,1]{1,0,2:T(8,128)}, f32[12,144,1]{1,0,2:T(8,128)}, f32[12,144,1]{1,0,2:T(8,128)}, f32[12,144,128]{2,1,0:T(8,128)}, /*ind...) while((s32[]{:T(128)}, f32[12,144,1]{1,0,2:T(8,128)}, ...), condition=%wide.region_8.9_spmd.clone, body=%wide.region_4.8_spmd.clone.sunk | while | flops 777973248 | bytes 86200160 | solution.py:182
  221.1 23.3 %collective-permute-done = bf16[4,144,1536]{2,1,0:T(8,128)(2,1)} collective-permute-done((bf16[4,144,1536]{2,1,0:T(8,128)(2,1)}, bf16[4,144,1536]{2,1,0:T(8,128)(2,1)}, u32[]{:S(2)}, u32[]{:S(2)}) %collective-permute-start) | collective-permute-done | bytes 1769504 | tf_op jit(solution)/shard_map/while/body/eval_jaxpr/ppermute | solution.py:21
  252.2 2.5 squeeze.23
  254.7 2.5 squeeze.21
  261.3 3.0 fusion.170
  269.5 6.1 collective-permute-done.1
  277.2 23.3 %collective-permute-done = bf16[4,144,1536]{2,1,0:T(8,128)(2,1)} collective-permute-done((bf16[4,144,1536]{2,1,0:T(8,128)(2,1)}, bf16[4,144,1536]{2,1,0:T(8,128)(2,1)}, u32[]{:S(2)}, u32[]{:S(2)}) %collective-permute-start) | collective-permute-done | bytes 1769504 | tf_op jit(solution)/shard_map/while/body/eval_jaxpr/ppermute | solution.py:21
  308.3 2.5 squeeze.23
  310.8 2.5 squeeze.21
  317.4 3.0 fusion.170
  325.6 6.1 collective-permute-done.1
  333.3 23.3 %collective-permute-done = bf16[4,144,1536]{2,1,0:T(8,128)(2,1)} collective-permute-done((bf16[4,144,1536]{2,1,0:T(8,128)(2,1)}, bf16[4,144,1536]{2,1,0:T(8,128)(2,1)}, u32[]{:S(2)}, u32[]{:S(2)}) %collective-permute-start) | collective-permute-done | bytes 1769504 | tf_op jit(solution)/shard_map/while/body/eval_jaxpr/ppermute | solution.py:21
  364.4 2.5 squeeze.23
  366.9 2.5 squeeze.21
  373.5 3.0 fusion.170
  381.7 6.1 collective-permute-done.1
  389.4 23.3 %collective-permute-done = bf16[4,144,1536]{2,1,0:T(8,128)(2,1)} collective-permute-done((bf16[4,144,1536]{2,1,0:T(8,128)(2,1)}, bf16[4,144,1536]{2,1,0:T(8,128)(2,1)}, u32[]{:S(2)}, u32[]{:S(2)}) %collective-permute-start) | collective-permute-done | bytes 1769504 | tf_op jit(solution)/shard_map/while/body/eval_jaxpr/ppermute | solution.py:21
  420.5 2.5 squeeze.23
  429.6 3.0 fusion.170
  437.8 6.1 collective-permute-done.1
  445.5 23.3 %collective-permute-done = bf16[4,144,1536]{2,1,0:T(8,128)(2,1)} collective-permute-done((bf16[4,144,1536]{2,1,0:T(8,128)(2,1)}, bf16[4,144,1536]{2,1,0:T(8,128)(2,1)}, u32[]{:S(2)}, u32[]{:S(2)}) %collective-permute-start) | collective-permute-done | bytes 1769504 | tf_op jit(solution)/shard_map/while/body/eval_jaxpr/ppermute | solution.py:21
  476.7 2.5 squeeze.23
  485.8 3.0 fusion.170
  494.0 6.1 collective-permute-done.1
  501.7 23.3 %collective-permute-done = bf16[4,144,1536]{2,1,0:T(8,128)(2,1)} collective-permute-done((bf16[4,144,1536]{2,1,0:T(8,128)(2,1)}, bf16[4,144,1536]{2,1,0:T(8,128)(2,1)}, u32[]{:S(2)}, u32[]{:S(2)}) %collective-permute-start) | collective-permute-done | bytes 1769504 | tf_op jit(solution)/shard_map/while/body/eval_jaxpr/ppermute | solution.py:21
  532.8 2.5 squeeze.23
  541.9 3.0 fusion.170
  550.1 6.1 collective-permute-done.1
  557.8 23.3 %collective-permute-done = bf16[4,144,1536]{2,1,0:T(8,128)(2,1)} collective-permute-done((bf16[4,144,1536]{2,1,0:T(8,128)(2,1)}, bf16[4,144,1536]{2,1,0:T(8,128)(2,1)}, u32[]{:S(2)}, u32[]{:S(2)}) %collective-permute-start) | collective-permute-done | bytes 1769504 | tf_op jit(solution)/shard_map/while/body/eval_jaxpr/ppermute | solution.py:21
  588.9 2.5 squeeze.23
  598.0 3.0 fusion.170
  606.2 6.1 collective-permute-done.1
  613.9 23.2 %collective-permute-done.2 = bf16[4,144,1536]{2,1,0:T(8,128)(2,1)S(1)} collective-permute-done((bf16[4,144,1536]{2,1,0:T(8,128)(2,1)}, bf16[4,144,1536]{2,1,0:T(8,128)(2,1)S(1)}, u32[]{:S(2)}, u32[]{:S(2)}) %collective-permute-start.2) | collective-permute-done | bytes 1769504 | tf_op jit(solution)/shard_map/ppermute | solution.py:21
  641.2 2.7 reshape_squeeze.19
  647.1 2.8 fusion.137
  649.8 2.6 reshape_squeeze.18
  652.4 2.5 reshape_squeeze.17
  655.7 2.5 convolution_add_fusion.2
  660.9 3.3 reduce.7
  665.1 3.5 all-to-all-start.7
  669.5 3.3 reduce.6
  674.7 3.5 all-to-all-start.6
  679.5 4.8 all-to-all-done.6
  (491 shorter events, 217.0 us)
Async XLA Ops:
  4.8 23.8 %copy-start.32 = (bf16[1,72,3072]{2,1,0:T(8,128)(2,1)S(1)}, bf16[1,72,3072]{2,1,0:T(8,128)(2,1)}, u32[]{:S(2)}) copy-start(bf16[1,72,3072]{2,1,0:T(8,128)(2,1)} %param.14) | copy-start | bytes 1327108
  24.1 111.9 %all-to-all-start = ((bf16[2,2,55296]{2,1,0:T(2,128)(2,1)}), bf16[2,2,55296]{2,1,0:T(2,128)(2,1)S(1)}, u32[]{:S(2)}, u32[]{:S(2)}) async-start(bf16[2,2,55296]{2,1,0:T(2,128)(2,1)} %reshape.176), calls=%async_computation | async-start | bytes 884736 | tf_op jit(solution)/shard_map/all_to_all | solution.py:84
  47.4 3.2 copy-start.33
  52.5 19.5 %copy-start.34 = (bf16[1,72,3072]{2,1,0:T(8,128)(2,1)S(1)}, bf16[1,72,3072]{2,1,0:T(8,128)(2,1)}, u32[]{:S(2)}) copy-start(bf16[1,72,3072]{2,1,0:T(8,128)(2,1)} %param.15) | copy-start | bytes 1327108
  73.9 19.7 %copy-start.35 = (bf16[1,72,3072]{2,1,0:T(8,128)(2,1)S(1)}, bf16[1,72,3072]{2,1,0:T(8,128)(2,1)}, u32[]{:S(2)}) copy-start(bf16[1,72,3072]{2,1,0:T(8,128)(2,1)} %param.10) | copy-start | bytes 1327108
  95.4 19.3 %copy-start.36 = (bf16[1,72,3072]{2,1,0:T(8,128)(2,1)S(1)}, bf16[1,72,3072]{2,1,0:T(8,128)(2,1)}, u32[]{:S(2)}) copy-start(bf16[1,72,3072]{2,1,0:T(8,128)(2,1)} %param.13) | copy-start | bytes 1327108
  136.8 12.1 %all-to-all-start.2 = ((bf16[2,2,55296]{2,1,0:T(2,128)(2,1)}), bf16[2,2,55296]{2,1,0:T(2,128)(2,1)}, u32[]{:S(2)}, u32[]{:S(2)}) async-start(bf16[2,2,55296]{2,1,0:T(2,128)(2,1)} %reshape.174), calls=%async_computation.2 | async-start | bytes 884736 | tf_op jit(solution)/shard_map/all_to_all | solution.py:87
  149.0 13.2 %all-to-all-start.1 = ((bf16[2,2,55296]{2,1,0:T(2,128)(2,1)}), bf16[2,2,55296]{2,1,0:T(2,128)(2,1)}, u32[]{:S(2)}, u32[]{:S(2)}) async-start(bf16[2,2,55296]{2,1,0:T(2,128)(2,1)} %reshape.178), calls=%async_computation.1 | async-start | bytes 884736 | tf_op jit(solution)/shard_map/all_to_all | solution.py:85
  161.2 4.6 copy-start.42
  162.1 10.7 %all-to-all-start.3 = ((bf16[2,2,55296]{2,1,0:T(2,128)(2,1)}), bf16[2,2,55296]{2,1,0:T(2,128)(2,1)S(1)}, u32[]{:S(2)}, u32[]{:S(2)}) async-start(bf16[2,2,55296]{2,1,0:T(2,128)(2,1)} %reshape.172), calls=%async_computation.3 | async-start | bytes 884736 | tf_op jit(solution)/shard_map/all_to_all | solution.py:88
  172.8 18.7 %all-to-all-start.4 = ((bf16[2,2,55296]{2,1,0:T(2,128)(2,1)}), bf16[2,2,55296]{2,1,0:T(2,128)(2,1)}, u32[]{:S(2)}, u32[]{:S(2)}) async-start(bf16[2,2,55296]{2,1,0:T(2,128)(2,1)} %reshape.180), calls=%async_computation.4 | async-start | bytes 884736 | tf_op jit(solution)/shard_map/all_to_all | solution.py:83
  191.5 11.7 %all-to-all-start.5 = ((bf16[2,2,55296]{2,1,0:T(2,128)(2,1)}), bf16[2,2,55296]{2,1,0:T(2,128)(2,1)}, u32[]{:S(2)}, u32[]{:S(2)}) async-start(bf16[2,2,55296]{2,1,0:T(2,128)(2,1)} %reshape.182), calls=%async_computation.5 | async-start | bytes 884736 | tf_op jit(solution)/shard_map/all_to_all | solution.py:86
  215.9 3.3 copy-start.30
  219.4 25.0 %collective-permute-start = (bf16[4,144,1536]{2,1,0:T(8,128)(2,1)}, bf16[4,144,1536]{2,1,0:T(8,128)(2,1)}, u32[]{:S(2)}, u32[]{:S(2)}) collective-permute-start(bf16[4,144,1536]{2,1,0:T(8,128)(2,1)} %get-tuple-element.245), channel_id=1, source_target_pairs={{15,0},{0,1},{1,2},{2,3},{3,4},{4,5},{5,6},{6,7},{7,8},{8,9},{9,10... | collective-permute-start | bytes 5308424 | tf_op jit(solution)/shard_map/while/body/eval_jaxpr/ppermute | solution.py:21
  250.6 25.0 %collective-permute-start.1 = (bf16[4,144,1536]{2,1,0:T(8,128)(2,1)}, bf16[4,144,1536]{2,1,0:T(8,128)(2,1)}, u32[]{:S(2)}, u32[]{:S(2)}) collective-permute-start(bf16[4,144,1536]{2,1,0:T(8,128)(2,1)} %collective-permute-done), channel_id=1, source_target_pairs={{15,0},{0,1},{1,2},{2,3},{3,4},{4,5},{5,6},{6,7},{7,8},{8,9},{9,10... | collective-permute-start | bytes 5308424 | tf_op jit(solution)/shard_map/while/body/eval_jaxpr/ppermute | solution.py:21
  261.2 3.8 copy-start.1
  261.3 3.8 copy-start.6
  261.3 3.8 copy-start.13
  269.5 6.1 copy-start.4
  275.6 25.0 %collective-permute-start = (bf16[4,144,1536]{2,1,0:T(8,128)(2,1)}, bf16[4,144,1536]{2,1,0:T(8,128)(2,1)}, u32[]{:S(2)}, u32[]{:S(2)}) collective-permute-start(bf16[4,144,1536]{2,1,0:T(8,128)(2,1)} %get-tuple-element.245), channel_id=1, source_target_pairs={{15,0},{0,1},{1,2},{2,3},{3,4},{4,5},{5,6},{6,7},{7,8},{8,9},{9,10... | collective-permute-start | bytes 5308424 | tf_op jit(solution)/shard_map/while/body/eval_jaxpr/ppermute | solution.py:21
  306.7 25.0 %collective-permute-start.1 = (bf16[4,144,1536]{2,1,0:T(8,128)(2,1)}, bf16[4,144,1536]{2,1,0:T(8,128)(2,1)}, u32[]{:S(2)}, u32[]{:S(2)}) collective-permute-start(bf16[4,144,1536]{2,1,0:T(8,128)(2,1)} %collective-permute-done), channel_id=1, source_target_pairs={{15,0},{0,1},{1,2},{2,3},{3,4},{4,5},{5,6},{6,7},{7,8},{8,9},{9,10... | collective-permute-start | bytes 5308424 | tf_op jit(solution)/shard_map/while/body/eval_jaxpr/ppermute | solution.py:21
  317.4 3.8 copy-start.1
  317.4 3.8 copy-start.6
  317.4 3.8 copy-start.13
  325.6 6.1 copy-start.4
  331.7 25.0 %collective-permute-start = (bf16[4,144,1536]{2,1,0:T(8,128)(2,1)}, bf16[4,144,1536]{2,1,0:T(8,128)(2,1)}, u32[]{:S(2)}, u32[]{:S(2)}) collective-permute-start(bf16[4,144,1536]{2,1,0:T(8,128)(2,1)} %get-tuple-element.245), channel_id=1, source_target_pairs={{15,0},{0,1},{1,2},{2,3},{3,4},{4,5},{5,6},{6,7},{7,8},{8,9},{9,10... | collective-permute-start | bytes 5308424 | tf_op jit(solution)/shard_map/while/body/eval_jaxpr/ppermute | solution.py:21
  362.8 25.0 %collective-permute-start.1 = (bf16[4,144,1536]{2,1,0:T(8,128)(2,1)}, bf16[4,144,1536]{2,1,0:T(8,128)(2,1)}, u32[]{:S(2)}, u32[]{:S(2)}) collective-permute-start(bf16[4,144,1536]{2,1,0:T(8,128)(2,1)} %collective-permute-done), channel_id=1, source_target_pairs={{15,0},{0,1},{1,2},{2,3},{3,4},{4,5},{5,6},{6,7},{7,8},{8,9},{9,10... | collective-permute-start | bytes 5308424 | tf_op jit(solution)/shard_map/while/body/eval_jaxpr/ppermute | solution.py:21
  373.5 3.8 copy-start.1
  373.5 3.8 copy-start.6
  373.5 3.8 copy-start.13
  381.7 6.1 copy-start.4
  387.8 25.0 %collective-permute-start = (bf16[4,144,1536]{2,1,0:T(8,128)(2,1)}, bf16[4,144,1536]{2,1,0:T(8,128)(2,1)}, u32[]{:S(2)}, u32[]{:S(2)}) collective-permute-start(bf16[4,144,1536]{2,1,0:T(8,128)(2,1)} %get-tuple-element.245), channel_id=1, source_target_pairs={{15,0},{0,1},{1,2},{2,3},{3,4},{4,5},{5,6},{6,7},{7,8},{8,9},{9,10... | collective-permute-start | bytes 5308424 | tf_op jit(solution)/shard_map/while/body/eval_jaxpr/ppermute | solution.py:21
  419.0 25.0 %collective-permute-start.1 = (bf16[4,144,1536]{2,1,0:T(8,128)(2,1)}, bf16[4,144,1536]{2,1,0:T(8,128)(2,1)}, u32[]{:S(2)}, u32[]{:S(2)}) collective-permute-start(bf16[4,144,1536]{2,1,0:T(8,128)(2,1)} %collective-permute-done), channel_id=1, source_target_pairs={{15,0},{0,1},{1,2},{2,3},{3,4},{4,5},{5,6},{6,7},{7,8},{8,9},{9,10... | collective-permute-start | bytes 5308424 | tf_op jit(solution)/shard_map/while/body/eval_jaxpr/ppermute | solution.py:21
  429.6 3.8 copy-start.1
  429.6 3.8 copy-start.6
  429.6 3.8 copy-start.13
  437.8 6.1 copy-start.4
  443.9 25.0 %collective-permute-start = (bf16[4,144,1536]{2,1,0:T(8,128)(2,1)}, bf16[4,144,1536]{2,1,0:T(8,128)(2,1)}, u32[]{:S(2)}, u32[]{:S(2)}) collective-permute-start(bf16[4,144,1536]{2,1,0:T(8,128)(2,1)} %get-tuple-element.245), channel_id=1, source_target_pairs={{15,0},{0,1},{1,2},{2,3},{3,4},{4,5},{5,6},{6,7},{7,8},{8,9},{9,10... | collective-permute-start | bytes 5308424 | tf_op jit(solution)/shard_map/while/body/eval_jaxpr/ppermute | solution.py:21
  475.1 25.0 %collective-permute-start.1 = (bf16[4,144,1536]{2,1,0:T(8,128)(2,1)}, bf16[4,144,1536]{2,1,0:T(8,128)(2,1)}, u32[]{:S(2)}, u32[]{:S(2)}) collective-permute-start(bf16[4,144,1536]{2,1,0:T(8,128)(2,1)} %collective-permute-done), channel_id=1, source_target_pairs={{15,0},{0,1},{1,2},{2,3},{3,4},{4,5},{5,6},{6,7},{7,8},{8,9},{9,10... | collective-permute-start | bytes 5308424 | tf_op jit(solution)/shard_map/while/body/eval_jaxpr/ppermute | solution.py:21
  485.7 3.8 copy-start.1
  485.7 3.8 copy-start.6
  485.7 3.8 copy-start.13
  494.0 6.1 copy-start.4
  500.0 25.0 %collective-permute-start = (bf16[4,144,1536]{2,1,0:T(8,128)(2,1)}, bf16[4,144,1536]{2,1,0:T(8,128)(2,1)}, u32[]{:S(2)}, u32[]{:S(2)}) collective-permute-start(bf16[4,144,1536]{2,1,0:T(8,128)(2,1)} %get-tuple-element.245), channel_id=1, source_target_pairs={{15,0},{0,1},{1,2},{2,3},{3,4},{4,5},{5,6},{6,7},{7,8},{8,9},{9,10... | collective-permute-start | bytes 5308424 | tf_op jit(solution)/shard_map/while/body/eval_jaxpr/ppermute | solution.py:21
  531.2 25.0 %collective-permute-start.1 = (bf16[4,144,1536]{2,1,0:T(8,128)(2,1)}, bf16[4,144,1536]{2,1,0:T(8,128)(2,1)}, u32[]{:S(2)}, u32[]{:S(2)}) collective-permute-start(bf16[4,144,1536]{2,1,0:T(8,128)(2,1)} %collective-permute-done), channel_id=1, source_target_pairs={{15,0},{0,1},{1,2},{2,3},{3,4},{4,5},{5,6},{6,7},{7,8},{8,9},{9,10... | collective-permute-start | bytes 5308424 | tf_op jit(solution)/shard_map/while/body/eval_jaxpr/ppermute | solution.py:21
  541.8 3.1 copy-start.28
  541.8 3.8 copy-start.1
  541.8 3.8 copy-start.6
  541.9 3.8 copy-start.13
  550.1 6.1 copy-start.4
  556.2 25.0 %collective-permute-start = (bf16[4,144,1536]{2,1,0:T(8,128)(2,1)}, bf16[4,144,1536]{2,1,0:T(8,128)(2,1)}, u32[]{:S(2)}, u32[]{:S(2)}) collective-permute-start(bf16[4,144,1536]{2,1,0:T(8,128)(2,1)} %get-tuple-element.245), channel_id=1, source_target_pairs={{15,0},{0,1},{1,2},{2,3},{3,4},{4,5},{5,6},{6,7},{7,8},{8,9},{9,10... | collective-permute-start | bytes 5308424 | tf_op jit(solution)/shard_map/while/body/eval_jaxpr/ppermute | solution.py:21
  587.3 25.0 %collective-permute-start.1 = (bf16[4,144,1536]{2,1,0:T(8,128)(2,1)}, bf16[4,144,1536]{2,1,0:T(8,128)(2,1)}, u32[]{:S(2)}, u32[]{:S(2)}) collective-permute-start(bf16[4,144,1536]{2,1,0:T(8,128)(2,1)} %collective-permute-done), channel_id=1, source_target_pairs={{15,0},{0,1},{1,2},{2,3},{3,4},{4,5},{5,6},{6,7},{7,8},{8,9},{9,10... | collective-permute-start | bytes 5308424 | tf_op jit(solution)/shard_map/while/body/eval_jaxpr/ppermute | solution.py:21
  598.0 3.8 copy-start.1
  598.0 3.8 copy-start.6
  598.0 3.8 copy-start.13
  606.2 6.1 copy-start.4
  612.3 24.9 %collective-permute-start.2 = (bf16[4,144,1536]{2,1,0:T(8,128)(2,1)}, bf16[4,144,1536]{2,1,0:T(8,128)(2,1)S(1)}, u32[]{:S(2)}, u32[]{:S(2)}) collective-permute-start(bf16[4,144,1536]{2,1,0:T(8,128)(2,1)} %get-tuple-element.56), channel_id=1, source_target_pairs={{15,0},{0,1},{1,2},{2,3},{3,4},{4,5},{5,6},{6,7},{7,8},{8,9},{9,10... | collective-permute-start | bytes 5308424 | tf_op jit(solution)/shard_map/ppermute | solution.py:21
  641.2 4.2 copy-start.19
  645.5 4.4 copy-start.37
  649.8 5.9 copy-start.7
  655.7 3.9 copy-start.40
  660.9 7.7 %copy-start.41 = (f32[12,144]{1,0:T(8,128)S(1)}, f32[12,144]{1,0:T(8,128)}, u32[]{:S(2)}) copy-start(f32[12,144]{1,0:T(8,128)} %copy-done.40) | copy-start | bytes 20740
  665.1 9.6 %all-to-all-start.7 = ((bf16[2,2,55296]{2,1,0:T(2,128)(2,1)}), bf16[2,2,55296]{2,1,0:T(2,128)(2,1)S(1)}, u32[]{:S(2)}, u32[]{:S(2)}) async-start(bf16[2,2,55296]{2,1,0:T(2,128)(2,1)} %reshape.186), calls=%async_computation.7 | async-start | bytes 884736 | tf_op jit(solution)/shard_map/all_to_all | solution.py:198
  674.7 9.6 %all-to-all-start.6 = ((bf16[2,2,55296]{2,1,0:T(2,128)(2,1)}), bf16[2,2,55296]{2,1,0:T(2,128)(2,1)S(1)}, u32[]{:S(2)}, u32[]{:S(2)}) async-start(bf16[2,2,55296]{2,1,0:T(2,128)(2,1)} %reshape.184), calls=%async_computation.6 | async-start | bytes 884736 | tf_op jit(solution)/shard_map/all_to_all | solution.py:197
  (94 other events, 187.6 us)
where the time goes:
time: 694 us; the launch traced here: 686 us
  waiting for transfers between devices  239 us (34%)
  local copies, waits for them, and re-layouts  200 us (29%)
  other arithmetic  138 us (20%)
  matrix products  73 us (11%)
  starting transfers between devices  32.3 us (5%)
    ppermute x15, waiting for transfers between devices, passed_along(): return lax.ppermute(block, axis, route)  229 us
    unnamed x13, other arithmetic  109 us
    unnamed x86, local copies, waits for them, and re-layouts  55.1 us
    squeeze x14, local copies, waits for them, and re-layouts, absorb_segment(): block_key_dot = key_block[2].reshape(count, heads_here, HD)  34.4 us
    dot_general x8, matrix products, absorb_segment(): jnp.einsum('qhd,khd->hqk', query_pair, key_pair, preferred_element_type=j...  24.1 us
    while x224, local copies, waits for them, and re-layouts  21.2 us
    squeeze x7, local copies, waits for them, and re-layouts, absorb_segment(): block_value_dot = key_block[3].reshape(count, heads_here, HD)  17.5 us
  transfers between devices with their start and end apart: 23, of which 19 were waited for; matrix products, arithmetic and copies ran while one was open for 43% of the time, Pallas kernels for 0%

commit v1 on v0

--- a/solution.py
+++ b/solution.py
@@ -1,8 +1,11 @@
+import functools
 import math
 
 import jax
 import jax.numpy as jnp
 from jax import lax
+from jax.experimental import pallas as pl
+from jax.experimental.pallas import tpu as pltpu
 from jax.sharding import PartitionSpec as P
 
 HD = 128
@@ -200,6 +203,312 @@
     return (returned[0], returned[1])
 
 
+MESH = pl.DeviceIdType.MESH
+ARRAYS = 4
+
+
+def prepare_kernel(q, k, v, qt, kt, vt, qg, kg, cos_ref, before_ref, after_ref, kv_out, q_out):
+    cosine, before, after = cos_ref[...], before_ref[...], after_ref[...]
+
+    def rotate(x):
+        return x * cosine + pltpu.roll(x, HD - 1, 1) * before + pltpu.roll(x, 1, 1) * after
+
+    def pair(raw, tangent, gain):
+        values = raw.astype(jnp.float32)
+        motion = tangent.astype(jnp.float32)
+        inverse = lax.rsqrt(jnp.mean(values * values, axis=-1, keepdims=True) + EPSILON)
+        coupling = jnp.mean(values * motion, axis=-1, keepdims=True)
+        normed = values * inverse * gain
+        moved = gain * (motion * inverse - values * (inverse * inverse * inverse * coupling))
+        return rotate(normed).astype(jnp.bfloat16), rotate(moved).astype(jnp.bfloat16)
+
+    for head in range(q.shape[1] // HD):
+        columns = slice(head * HD, (head + 1) * HD)
+        q_hat, q_dot = pair(q[:, columns], qt[:, columns], qg[...])
+        k_hat, k_dot = pair(k[:, columns], kt[:, columns], kg[...])
+        q_out[head, 0] = q_hat
+        q_out[head, 1] = q_dot
+        kv_out[head, 0] = k_hat
+        kv_out[head, 1] = k_dot
+        kv_out[head, 2] = v[:, columns]
+        kv_out[head, 3] = vt[:, columns]
+
+
+def prepare(arrays, gains, tables, heads_each):
+    rows, width = arrays[0].shape
+    heads = width // HD
+    block = pl.BlockSpec((rows, heads_each * HD), lambda i: (0, i))
+    gain = pl.BlockSpec((1, HD), lambda i: (0, 0))
+    table = pl.BlockSpec((rows, HD), lambda i: (0, 0))
+    return pl.pallas_call(
+        prepare_kernel,
+        grid=(heads // heads_each,),
+        in_specs=[block] * 6 + [gain] * 2 + [table] * 3,
+        out_specs=[
+            pl.BlockSpec((heads_each, ARRAYS, rows, HD), lambda i: (i, 0, 0, 0)),
+            pl.BlockSpec((heads_each, 2, rows, HD), lambda i: (i, 0, 0, 0)),
+        ],
+        out_shape=[
+            jax.ShapeDtypeStruct((heads, ARRAYS, rows, HD), jnp.bfloat16),
+            jax.ShapeDtypeStruct((heads, 2, rows, HD), jnp.bfloat16),
+        ],
+        compiler_params=pltpu.CompilerParams(dimension_semantics=("arbitrary",)),
+    )(*arrays, *gains, *tables)
+
+
+def joint_kernel(
+    n_head, ring, heads_each, rows,
+    kv_ref, q_ref, out_ref,
+    kv_held, q_held, sent, peak_s, total_s, drift_s, sum_s, dot_s,
+    kv_send, kv_recv, pass_send, pass_recv, q_send, q_recv, o_send, o_recv,
+):
+    chips = n_head * ring
+    y = lax.axis_index("head")
+    n = lax.axis_index("blk")
+    core = n % 2
+    half = n // (2 * ring)
+    r = (n // 2) % ring
+    group = y * ring + r
+
+    def chip(offset, far):
+        return (y + offset // ring) % n_head, (r + offset % ring) % ring, (half + far) % 2
+
+    def device(offset, far):
+        ty, tr, th = chip(offset, far)
+        return (ty, (th * ring + tr) * 2 + core)
+
+    def source(offset):
+        ty = (y + n_head - offset // ring) % n_head
+        tr = (r + ring - offset % ring) % ring
+        return ty, tr, (ty, (half * ring + tr) * 2 + core)
+
+    partner = (y, (half * ring + r) * 2 + 1 - core)
+
+    barrier = pltpu.get_barrier_semaphore()
+    for far in range(2):
+        for offset in range(chips):
+            if far or offset:
+                pl.semaphore_signal(barrier, inc=1, device_id=device(offset, far), device_id_type=MESH)
+    pl.semaphore_signal(barrier, inc=1, device_id=partner, device_id_type=MESH)
+    pl.semaphore_wait(barrier, 2 * chips)
+
+    def kv_copy(j, offset, far):
+        ty, tr, _ = chip(offset, far)
+        return pltpu.make_async_remote_copy(
+            src_ref=kv_ref.at[(ty * ring + tr) * heads_each + j],
+            dst_ref=kv_held.at[far, j, :, pl.ds(pl.multiple_of(offset * 2 * rows, 8), rows), :],
+            send_sem=kv_send.at[far, j, offset],
+            recv_sem=kv_recv.at[far, j, offset],
+            device_id=device(offset, far),
+            device_id_type=MESH,
+        )
+
+    def pass_copy(j, offset, far):
+        slot = kv_held.at[far, j, :, pl.ds(pl.multiple_of(offset * 2 * rows, 8), rows), :]
+        own = isinstance(offset, int) and offset == 0 and far == 0
+        return pltpu.make_async_remote_copy(
+            src_ref=kv_ref.at[group * heads_each + j] if own else slot,
+            dst_ref=kv_held.at[far, j, :, pl.ds(pl.multiple_of((offset * 2 + 1) * rows, 8), rows), :],
+            send_sem=pass_send.at[far, j, offset],
+            recv_sem=pass_recv.at[far, j, offset],
+            device_id=partner,
+            device_id_type=MESH,
+        )
+
+    def q_copy(offset):
+        ty, tr, _ = chip(offset, 0)
+        return pltpu.make_async_remote_copy(
+            src_ref=q_ref.at[pl.ds((ty * ring + tr) * heads_each, heads_each)],
+            dst_ref=q_held.at[:, :, pl.ds(pl.multiple_of(offset * rows, 8), rows), :],
+            send_sem=q_send.at[offset],
+            recv_sem=q_recv.at[offset],
+            device_id=device(offset, 0),
+            device_id_type=MESH,
+        )
+
+    def o_copy(j, offset):
+        _, _, there = source(offset)
+        return pltpu.make_async_remote_copy(
+            src_ref=sent.at[j, :, pl.ds(pl.multiple_of(offset * rows, 8), rows), :],
+            dst_ref=out_ref.at[group * heads_each + j],
+            send_sem=o_send.at[j, offset],
+            recv_sem=o_recv.at[j, offset],
+            device_id=there,
+            device_id_type=MESH,
+        )
+
+    def each(low, body):
+        @pl.loop(low, chips)
+        def _(offset):
+            body(offset)
+
+    def start_kv(j, far):
+        each(1 - far, lambda offset: kv_copy(j, offset, far).start())
+
+    start_kv(0, 1)
+    each(1, lambda offset: q_copy(offset).start())
+    start_kv(0, 0)
+    for j in range(heads_each):
+        pass_copy(j, 0, 0).start()
+    for j in range(1, heads_each):
+        start_kv(j, 1)
+        start_kv(j, 0)
+    mine = pl.ds(group * heads_each, heads_each)
+    q_held[:, :, 0:rows, :] = q_ref[mine]
+    kv_held[0, :, :, 0:rows, :] = kv_ref[mine]
+
+    scale = 1.0 / math.sqrt(HD)
+    keys = 2 * chips * rows
+    tile = 2 * rows
+
+    def arrive(j, far):
+        def step(offset):
+            kv_copy(j, offset, far).wait_recv()
+            pass_copy(j, offset, far).start()
+
+        each(1 - far, step)
+
+    def attend(j, far):
+        if far == 0:
+            pass_copy(j, 0, 0).wait_recv()
+        each(1 - far, lambda offset: pass_copy(j, offset, far).wait_recv())
+
+        @pl.loop(0, chips * rows // tile)
+        def _(t):
+            at = pl.ds(pl.multiple_of(t * tile, tile), tile)
+            q_hat = q_held[j, 0, at, :]
+            q_dot = q_held[j, 1, at, :]
+            k_hat, k_dot = kv_held[far, j, 0], kv_held[far, j, 1]
+            v, v_dot = kv_held[far, j, 2], kv_held[far, j, 3]
+            dims = (((1,), (1,)), ((), ()))
+            scores = lax.dot_general(q_hat, k_hat, dims, preferred_element_type=jnp.float32) * scale
+            moved = lax.dot_general(
+                jnp.concatenate([q_dot, q_hat], axis=1),
+                jnp.concatenate([k_hat, k_dot], axis=1),
+                dims,
+                preferred_element_type=jnp.float32,
+            ) * scale
+            peak = jnp.max(scores, axis=1, keepdims=True)
+            if far:
+                old = peak_s[at, :1]
+                peak = jnp.maximum(peak, old)
+            weights = jnp.exp(scores - peak)
+            product = weights * moved
+            total = jnp.sum(weights, axis=1, keepdims=True)
+            drift = jnp.sum(product, axis=1, keepdims=True)
+            low = weights.astype(jnp.bfloat16)
+            both = jnp.dot(low, jnp.concatenate([v, v_dot], axis=1), preferred_element_type=jnp.float32)
+            summed = both[:, :HD]
+            summed_dot = both[:, HD:] + jnp.dot(
+                product.astype(jnp.bfloat16), v, preferred_element_type=jnp.float32
+            )
+            if far:
+                again = jnp.exp(old - peak)
+                total = total + again * total_s[at, :1]
+                drift = drift + again * drift_s[at, :1]
+                summed = summed + again * sum_s[at, :]
+                summed_dot = summed_dot + again * dot_s[at, :]
+                sent[j, 0, at, :] = (summed / total).astype(jnp.bfloat16)
+                sent[j, 1, at, :] = ((summed_dot - (drift / total) * summed) / total).astype(jnp.bfloat16)
+            else:
+                peak_s[at, :] = jnp.broadcast_to(peak, (tile, HD))
+                total_s[at, :] = jnp.broadcast_to(total, (tile, HD))
+                drift_s[at, :] = jnp.broadcast_to(drift, (tile, HD))
+                sum_s[at, :] = summed
+                dot_s[at, :] = summed_dot
+
+    each(1, lambda offset: q_copy(offset).wait_recv())
+    stages = [(j, far) for j in range(heads_each) for far in range(2)]
+    arrive(*stages[0])
+    for index, (j, far) in enumerate(stages):
+        if index + 1 < len(stages) and far == 0:
+            attend(j, far)
+            arrive(*stages[index + 1])
+        elif index + 1 < len(stages):
+            arrive(*stages[index + 1])
+            attend(j, far)
+        else:
+            attend(j, far)
+        if far:
+            each(1, lambda offset: o_copy(j, offset).start())
+            out_ref[group * heads_each + j] = sent[j, :, 0:rows, :]
+
+    for j in range(heads_each):
+        for far in range(2):
+            each(1 - far, lambda offset: kv_copy(j, offset, far).wait_send())
+            if far == 0:
+                pass_copy(j, 0, 0).wait_send()
+            each(1 - far, lambda offset: pass_copy(j, offset, far).wait_send())
+    each(1, lambda offset: q_copy(offset).wait_send())
+    for j in range(heads_each):
+        each(1, lambda offset: o_copy(j, offset).wait_send())
+
+    for j in range(heads_each):
+        each(1, lambda offset: o_copy(j, offset).wait_recv())
+
+
+def exchange(
+    query_rows, key_rows, value_rows, query_tangent, key_tangent, value_tangent, query_gain, key_gain
+):
+    n_head, n_blk = lax.axis_size("head"), lax.axis_size("blk")
+    rows, width = query_rows.shape[1:]
+    ring = n_blk // 4
+    chips = n_head * ring
+    heads = width // HD
+    heads_each = heads // chips
+    first = lax.axis_index("blk") * rows * n_head + lax.axis_index("head") * rows
+    cosine, sine = rotation(first, rows, HD)
+    even = (jnp.arange(HD) % 2 == 0)[None, :]
+    tables = (cosine, jnp.where(even, -sine, 0.0), jnp.where(even, 0.0, sine))
+    arrays = [a[0] for a in (query_rows, key_rows, value_rows, query_tangent, key_tangent, value_tangent)]
+    kv, q = prepare(arrays, (query_gain[None], key_gain[None]), tables, heads_each)
+    dma = pltpu.SemaphoreType.DMA
+    queries = chips * rows
+    vmem = pl.BlockSpec(memory_space=pltpu.VMEM)
+    out = pl.pallas_call(
+        functools.partial(joint_kernel, n_head, ring, heads_each, rows),
+        out_shape=jax.ShapeDtypeStruct((heads, 2, rows, HD), jnp.bfloat16),
+        in_specs=[vmem, vmem],
+        out_specs=vmem,
+        scratch_shapes=[
+            pltpu.VMEM((2, heads_each, ARRAYS, 2 * queries, HD), jnp.bfloat16),
+            pltpu.VMEM((heads_each, 2, queries, HD), jnp.bfloat16),
+            pltpu.VMEM((heads_each, 2, queries, HD), jnp.bfloat16),
+            pltpu.VMEM((queries, HD), jnp.float32),
+            pltpu.VMEM((queries, HD), jnp.float32),
+            pltpu.VMEM((queries, HD), jnp.float32),
+            pltpu.VMEM((queries, HD), jnp.float32),
+            pltpu.VMEM((queries, HD), jnp.float32),
+            dma((2, heads_each, chips)),
+            dma((2, heads_each, chips)),
+            dma((2, heads_each, chips)),
+            dma((2, heads_each, chips)),
+            dma((chips,)),
+            dma((chips,)),
+            dma((heads_each, chips)),
+            dma((heads_each, chips)),
+        ],
+        compiler_params=pltpu.CompilerParams(
+            collective_id=0, has_side_effects=True, vmem_limit_bytes=60 * 1024 * 1024
+        ),
+    )(kv, q)
+    flat = out.transpose(1, 2, 0, 3).reshape(2, 1, rows, width)
+    return flat[0], flat[1]
+
+
+def chosen(mesh):
+    n_head, n_blk = mesh.shape["head"], mesh.shape["blk"]
+
+    def run(*arrays):
+        heads = arrays[0].shape[2] // HD
+        rows = arrays[0].shape[1]
+        if n_blk == GROUP and heads % (n_head * n_blk // 4) == 0 and rows % 8 == 0:
+            return exchange(*arrays)
+        return local(*arrays)
+
+    return run
+
+
 def solution(mesh):
     in_specs = (
         P("blk", "head", None),
@@ -212,4 +521,4 @@
         P(),
     )
     out_specs = (P("blk", "head", None), P("blk", "head", None))
-    return jax.shard_map(local, mesh=mesh, in_specs=in_specs, out_specs=out_specs, check_vma=False)
+    return jax.shard_map(chosen(mesh), mesh=mesh, in_specs=in_specs, out_specs=out_specs, check_vma=False)

time: 694 us -> 119 us (0.17); the launches traced: 686 us -> 119 us
  waiting for transfers between devices: 239 us -> 0 us
  local copies, waits for them, and re-layouts: 200 us -> 3.75 us
  other arithmetic: 138 us -> 0.94 us
  Pallas kernels: 0 us -> 113 us
  matrix products: 73 us -> 0 us
  starting transfers between devices: 32.3 us -> 0 us
    ppermute x15 -> x0, waiting for transfers between devices: 229 us -> none  [passed_along(): return lax.ppermute(block, axis, route)]
    pallas_call x0 -> x2, Pallas kernels: none -> 113 us  [the longest x1 104 us: exchange(): pl.pallas_call(functools.partial(joint_kernel, n_head, ring, heads_each,...]
    unnamed x13 -> x0, other arithmetic: 109 us -> none
    dot_general x44 -> x0, matrix products: 73 us -> none  [the longest x8 24.1 us: absorb_segment(): jnp.einsum('qhd,khd->hqk', query_pair, key_pair, preferred_element_type=j...]
    squeeze x42 -> x2, local copies, waits for them, and re-layouts: 69.2 us -> 1.7 us  [exchange(): return (flat[0], flat[1])]
    unnamed x86 -> x1, local copies, waits for them, and re-layouts: 55.1 us -> 1.23 us
    all_to_all x8 -> x0, starting transfers between devices: 32.2 us -> none  [the longest x1 4.6 us: local(): lax.all_to_all(query_tangent, 'head', split_axis=2, concat_axis=1, tiled=...]
    while x224 -> x0, local copies, waits for them, and re-layouts: 21.2 us -> none
  transfers between devices with their start and end apart: 23 -> 0, of which waited for: 19 -> 0; matrix products, arithmetic and copies ran while one was open for 43% -> 0% of each run, Pallas kernels for 0% -> 0%
where the time goes in v1:
time: 119 us
  Pallas kernels  113 us (95%)
  local copies, waits for them, and re-layouts  3.75 us (3%)
    pallas_call x1, Pallas kernels, exchange(): pl.pallas_call(functools.partial(joint_kernel, n_head, ring, heads_each,...  104 us
    pallas_call x1, Pallas kernels, prepare(): pl.pallas_call(prepare_kernel, grid=(heads // heads_each,), in_specs=[blo...  9.35 us

profile of v1, /device:TPU:0, one launch (start us, length us, event | category | flops | bytes accessed | tf_op | source)
XLA Modules:
  0.0 118.8 jit_solution(6655431733618269105)
XLA Ops:
  0.7 0.1 broadcast_multiply_fusion.1
  0.8 0.2 fusion
  1.0 0.1 copy.10
  1.1 0.6 broadcast_select_fusion
  1.8 0.7 copy.12.cos_ref
  2.5 9.4 %shard_map.95 = (bf16[24,4,72,128]{3,2,1,0:T(8,128)(2,1)}, bf16[24,2,72,128]{3,2,1,0:T(8,128)(2,1)}) custom-call(bf16[72,3072]{1,0:T(8,128)(2,1)} %bitcast.22, bf16[72,3072]{1,0:T(8,128)(2,1)} %bitcast.23, bf16[72,3072]{1,0:T(8,128)(2,1)} %bitcast.24, bf16[72,3072]{1,0:T(8,128)(2,1)} %bitcast.25, bf16[72,3072]{1,0:T(8,128)(2,1)} %bitcast.26, ...), custom_call_target="tpu_custom_call" | custom-call | tf_op jit(solution)/shard_map/pallas_call | solution.py:243
  11.8 104.0 %shard_map.96 = bf16[24,2,72,128]{3,2,1,0:T(8,128)(2,1)} custom-call(bf16[24,4,72,128]{3,2,1,0:T(8,128)(2,1)} %get-tuple-element.4.kv_ref, bf16[24,2,72,128]{3,2,1,0:T(8,128)(2,1)} %get-tuple-element.5.q_ref), custom_call_target="tpu_custom_call" | custom-call | tf_op jit(solution)/shard_map/pallas_call | solution.py:468
  115.8 1.2 %slice_bitcast_fusion = (bf16[24,1,9,8,128]{4,3,2,1,0:T(8,128)(2,1)S(1)}, bf16[24,1,9,8,128]{4,3,2,1,0:T(8,128)(2,1)S(1)}) fusion(bf16[2,72,24,128]{3,1,0,2:T(8,128)(2,1)} %bitcast.21), kind=kLoop, calls=%fused_computation.2 | loop fusion | bytes 1769472
  117.1 0.9 copy.19
  117.9 0.9 copy.20
  (7 shorter events, 0.1 us)
